TPU v7x, 32 devices: a whole 2x2x4 slice. The times are simulated.
32 devices in a mesh: grp: 8 (over z, y), blk: 4 (over x, core).
Axes of the slice: x: 2, y: 2, z: 4, core: 2. Of those that a mesh axis runs over, the one named last changes fastest.
Arguments:
- query: bfloat16 [4096, 512], P(('grp', 'blk')), may hold values from -6 to 6
- key: bfloat16 [4096, 512], P(('grp', 'blk')), may hold values from -6 to 6
- value: bfloat16 [4096, 512], P(('grp', 'blk')), may hold values from -6 to 6
- gate_u: bfloat16 [4096, 512], P(('grp', 'blk')), may hold values from -6 to 6
- out_grad: bfloat16 [4096, 1024], P(('grp', 'blk')), may hold values from -6 to 6
- lengths: int32 [8], P('grp'), may hold values from 32 to 512
- norm_gain: float32 [512], replicated, may hold values from 0.1 to 1.9
- out_weight: bfloat16 [512, 1024], replicated, may hold values from -0.25 to 0.25
Outputs:
- layer_out: bfloat16 [4096, 1024], P(('grp', 'blk'))
- grad_query: bfloat16 [4096, 512], P(('grp', 'blk'))
- grad_key: bfloat16 [4096, 512], P(('grp', 'blk'))
- grad_value: bfloat16 [4096, 512], P(('grp', 'blk'))
- grad_gate: bfloat16 [4096, 512], P(('grp', 'blk'))
- grad_weight: float32 [512, 1024], P(None, 'blk')
Inputs may be any that keep to these rules, and one draw needn't show every extreme that they name: `lengths`: events of a user at or past its length are padding.
All inputs are finite; a program needn't handle non-finite values.
Results may differ from a plain program's by a relative error of at most 0.009.
Values may be sent and summed in bfloat16 or wider, within the bound.
No kernel may reach another device: no remote copies, remote signals or barrier semaphores. Data moves between devices by JAX's collectives and lax.ppermute only.
A program may use at most 64 MiB of HBM per device.

v0:
```python
import math
import jax
import jax.numpy as jnp
from jax import lax
from jax.sharding import PartitionSpec as P

HEADS = 8
HEAD = 64
EPS = 1e-05


def causal_mask(query_pos, key_pos, length):
    return (
        (key_pos[None, :] <= query_pos[:, None])
        & (query_pos[:, None] < length)
        & (key_pos[None, :] < length)
    )


def over_blocks(total_rows, step_fn, initial):
    size = math.gcd(total_rows, 512)

    def advance(index, carry):
        return step_fn(carry, index * size, size)

    return lax.fori_loop(0, total_rows // size, advance, initial)


def shards(query, key, value, gate_u, out_grad, lengths, norm_gain, out_weight):
    rows = query.shape[0]
    scale = HEAD ** (-0.5)
    length = lengths[0]
    lanes = lax.axis_size("blk")
    position = lax.axis_index("blk")
    first_row = position * rows
    row_pos = first_row + jnp.arange(rows, dtype=jnp.int32)
    total_len = rows * lanes
    query_heads = query.reshape(rows, HEADS, HEAD)
    key_heads = key.reshape(rows, HEADS, HEAD)
    value_heads = value.reshape(rows, HEADS, HEAD)
    zeros = jnp.zeros((rows, HEADS, HEAD), jnp.float32)
    keys_all, values_all = (
        lax.all_gather(key, "blk", axis=0, tiled=True),
        lax.all_gather(value, "blk", axis=0, tiled=True),
    )

    def forward_step(carry, begin, size):
        key_block = lax.dynamic_slice_in_dim(keys_all, begin, size, 0).reshape(size, HEADS, HEAD)
        value_block = lax.dynamic_slice_in_dim(values_all, begin, size, 0).reshape(
            size, HEADS, HEAD
        )
        scores = (
            jnp.einsum("rhd,nhd->hrn", query_heads, key_block, preferred_element_type=jnp.float32)
            * scale
        )
        mask = causal_mask(row_pos, begin + jnp.arange(size, dtype=jnp.int32), length)
        weights = (jax.nn.silu(scores) * mask[None]).astype(jnp.bfloat16)
        return carry + jnp.einsum(
            "hrn,nhd->rhd", weights, value_block, preferred_element_type=jnp.float32
        )

    attended = over_blocks(total_len, forward_step, zeros).reshape(rows, HEADS * HEAD)
    centre = attended - jnp.mean(attended, axis=1, keepdims=True)
    inv_std = lax.rsqrt(jnp.mean(centre * centre, axis=1, keepdims=True) + EPS)
    normed = centre * inv_std
    scaled = normed * norm_gain
    gates = gate_u.astype(jnp.float32)
    mixed = (scaled * gates).astype(jnp.bfloat16)
    layer_out = jnp.dot(mixed, out_weight, preferred_element_type=jnp.float32).astype(jnp.bfloat16)
    mixed_grad = lax.dot_general(
        out_grad, out_weight, (((1,), (1,)), ((), ())), preferred_element_type=jnp.float32
    )
    grad_gate = (mixed_grad * scaled).astype(jnp.bfloat16)
    normed_grad = mixed_grad * gates * norm_gain
    attended_grad = inv_std * (
        normed_grad
        - jnp.mean(normed_grad, axis=1, keepdims=True)
        - normed * jnp.mean(normed_grad * normed, axis=1, keepdims=True)
    )
    attended_grad = attended_grad.astype(jnp.bfloat16)
    grad_heads = attended_grad.reshape(rows, HEADS, HEAD)
    weight_term = lax.dot_general(
        mixed, out_grad, (((0,), (0,)), ((), ())), preferred_element_type=jnp.float32
    )

    def query_step(carry, begin, size):
        key_block = lax.dynamic_slice_in_dim(keys_all, begin, size, 0).reshape(size, HEADS, HEAD)
        value_block = lax.dynamic_slice_in_dim(values_all, begin, size, 0).reshape(
            size, HEADS, HEAD
        )
        scores = (
            jnp.einsum("rhd,nhd->hrn", query_heads, key_block, preferred_element_type=jnp.float32)
            * scale
        )
        mask = causal_mask(row_pos, begin + jnp.arange(size, dtype=jnp.int32), length)
        sigma = jax.nn.sigmoid(scores)
        prob_grad = jnp.einsum(
            "rhd,nhd->hrn", grad_heads, value_block, preferred_element_type=jnp.float32
        )
        score_grad = (prob_grad * sigma * (1.0 + scores * (1.0 - sigma)) * mask[None]).astype(
            jnp.bfloat16
        )
        return carry + jnp.einsum(
            "hrn,nhd->rhd", score_grad, key_block, preferred_element_type=jnp.float32
        )

    grad_query = (
        (over_blocks(total_len, query_step, zeros) * scale)
        .reshape(rows, HEADS * HEAD)
        .astype(jnp.bfloat16)
    )
    query_piece = lax.all_gather(query, "blk", axis=0, tiled=True)
    grad_piece = lax.all_gather(attended_grad, "blk", axis=0, tiled=True)
    count = query_piece.shape[0]

    def inner(acc, begin, size):
        key_acc, value_acc = acc
        query_block = lax.dynamic_slice_in_dim(query_piece, begin, size, 0).reshape(
            size, HEADS, HEAD
        )
        grad_block = lax.dynamic_slice_in_dim(grad_piece, begin, size, 0).reshape(size, HEADS, HEAD)
        scores = (
            jnp.einsum("nhd,rhd->hnr", query_block, key_heads, preferred_element_type=jnp.float32)
            * scale
        )
        mask = causal_mask(begin + jnp.arange(size, dtype=jnp.int32), row_pos, length)
        weights = (jax.nn.silu(scores) * mask[None]).astype(jnp.bfloat16)
        sigma = jax.nn.sigmoid(scores)
        prob_grad = jnp.einsum(
            "nhd,rhd->hnr", grad_block, value_heads, preferred_element_type=jnp.float32
        )
        score_grad = (prob_grad * sigma * (1.0 + scores * (1.0 - sigma)) * mask[None]).astype(
            jnp.bfloat16
        )
        key_acc = key_acc + jnp.einsum(
            "hnr,nhd->rhd", score_grad, query_block, preferred_element_type=jnp.float32
        )
        value_acc = value_acc + jnp.einsum(
            "hnr,nhd->rhd", weights, grad_block, preferred_element_type=jnp.float32
        )
        return (key_acc, value_acc)

    key_acc, value_acc = over_blocks(count, inner, (zeros, zeros))
    grad_key = (key_acc * scale).reshape(rows, HEADS * HEAD).astype(jnp.bfloat16)
    grad_value = value_acc.reshape(rows, HEADS * HEAD).astype(jnp.bfloat16)
    column_part = lax.psum_scatter(weight_term, "blk", scatter_dimension=1, tiled=True)
    grad_weight = lax.psum(column_part, "grp")
    return (layer_out, grad_query, grad_key, grad_value, grad_gate, grad_weight)


def solution(mesh):
    return jax.shard_map(
        shards,
        mesh=mesh,
        in_specs=(
            P(("grp", "blk"), None),
            P(("grp", "blk"), None),
            P(("grp", "blk"), None),
            P(("grp", "blk"), None),
            P(("grp", "blk"), None),
            P("grp"),
            P(),
            P(),
        ),
        out_specs=(
            P(("grp", "blk"), None),
            P(("grp", "blk"), None),
            P(("grp", "blk"), None),
            P(("grp", "blk"), None),
            P(("grp", "blk"), None),
            P(None, "blk"),
        ),
        check_vma=False,
    )
```

profile of v0, /device:TPU:0, one launch (start us, length us, event | category | flops | bytes accessed | tf_op | source)
XLA Modules:
  0.0 158.3 jit_solution(8994347896110078273)
XLA Ops:
  7.2 0.0 copy-start
  7.2 0.0 reduce-scatter.2.cloned.1.call-start
  7.2 9.0 %all_gather.13 = bf16[512,512]{1,0:T(8,128)(2,1)S(1)} all-gather(bf16[128,512]{1,0:T(8,128)(2,1)} %param.10), channel_id=1, replica_groups=mesh['grp'=8,'blk'=4] {'blk'}, dimensions={0}, use_global_device_ids=true | all-gather | bytes 655360 | tf_op jit(solution)/shard_map/all_gather | solution.py:44
  16.2 1.0 copy.26
  17.2 1.0 copy.24
  18.3 7.5 %all_gather.12 = bf16[512,512]{1,0:T(8,128)(2,1)S(1)} all-gather(bf16[128,512]{1,0:T(8,128)(2,1)} %param.9), channel_id=1, replica_groups=mesh['grp'=8,'blk'=4] {'blk'}, dimensions={0}, use_global_device_ids=true | all-gather | bytes 655360 | tf_op jit(solution)/shard_map/all_gather | solution.py:43
  25.7 1.0 copy.25
  27.5 1.5 fusion.33
  29.0 0.1 fusion.19
  29.1 0.0 copy-start.9
  29.1 0.0 copy-start.12
  29.1 2.0 %fusion.32 = (f32[128]{0:T(128)S(1)}, f32[8,128,64]{1,2,0:T(8,128)S(1)}) fusion(bf16[512,8,64]{0,2,1:T(8,128)(2,1)} %bitcast.51, f32[8,128,512]{2,1,0:T(8,128)S(1)} %fusion.33, f32[128,512]{1,0:T(8,128)S(1)} %fusion.19), kind=kOutput, calls=%fused_computation.56 | convolution fusion | flops 70844288 | bytes 3146240 | tf_op jit(solution)/shard_map/while/body/eval_jaxpr/hrn,nhd->rhd/dot_general | solution.py:58
  31.2 0.0 copy-done.13
  31.2 0.0 copy-done.10
  31.2 0.0 copy-start.4
  31.2 0.1 fusion.16
  31.3 0.5 add_rsqrt_fusion
  31.8 0.1 copy-done.4
  31.9 1.1 copy.27
  33.0 0.0 copy-start.3
  33.0 1.6 %fusion.23 = (f32[128]{0:T(128)S(1)}, f32[128]{0:T(128)S(1)}, f32[128,512]{1,0:T(8,128)S(1)}) fusion(f32[512]{0:T(512)S(1)} %copy-done.12, bf16[128,512]{1,0:T(8,128)(2,1)S(1)} %copy-done.9, f32[128]{0:T(128)} %add_rsqrt_fusion, f32[128,512]{1,0:T(8,128)S(1)} %copy.27, f32[128]{0:T(128)S(1)} %broadcast_multiply_fusion.2, bf16[128,1024]{1,0:T(8,128)(2,1)} %param.12, ...), kind=kOutput, calls=%fused_computation.40 | convolution fusion | flops 134741760 | bytes 1970176 | tf_op jit(solution)/shard_map/dot_general | solution.py:70
  34.6 1.8 %multiply_convert_fusion.6 = (bf16[128,512]{1,0:T(8,128)(2,1)}, bf16[128,512]{1,0:T(8,128)(2,1)S(1)}, bf16[128,512]{1,0:T(8,128)(2,1)S(1)}) fusion(f32[128,512]{1,0:T(8,128)S(1)} %get-tuple-element.96, f32[128,512]{1,0:T(8,128)S(1)} %copy.27, f32[512]{0:T(512)S(1)} %copy-done.12, f32[128]{0:T(128)} %add_rsqrt_fusion, f32[128]{0:T(128)S(1)} %broadcast_multiply_fusion.2, ...), kind=kLoop, calls=%fused_computation.28 | loop fusion | flops 983040 | bytes 1052672 | tf_op jit(solution)/shard_map/convert_element_type | solution.py:73
  36.4 0.6 copy-done.1
  37.0 1.8 %fusion.35 = f32[512,1024]{1,0:T(8,128)} fusion(bf16[128,512]{1,0:T(8,128)(2,1)S(1)} %get-tuple-element.93, bf16[128,1024]{1,0:T(8,128)(2,1)S(1)} %copy-done.3), kind=kOutput, calls=%fused_computation.59 | convolution fusion | flops 134217728 | bytes 2490368 | tf_op jit(solution)/shard_map/dot_general | solution.py:82
  38.9 0.0 reduce-scatter.2.cloned.1.call-update
  38.9 0.0 all-reduce.2.cloned.1.call-start
  38.9 0.8 copy.32
  39.7 0.7 copy.30
  40.4 0.1 copy.28
  40.6 0.0 copy-start.7
  40.6 3.3 %fusion.5 = bf16[8,128,64]{1,2,0:T(8,128)(2,1)} fusion(bf16[512,8,64]{0,2,1:T(8,128)(2,1)} %bitcast.47, f32[8,128,512]{2,1,0:T(8,128)S(1)} %fusion.33, bf16[128,8,64]{0,2,1:T(8,128)(2,1)S(1)} %bitcast.59, bf16[512,8,64]{0,2,1:T(8,128)(2,1)} %bitcast.52, f32[128,512]{1,0:T(8,128)} %copy-done.10), kind=kOutput, calls=%fused_computation.12 | convolution fusion | flops 140115968 | bytes 3670016 | tf_op jit(solution)/shard_map/while/body/eval_jaxpr/hrn,nhd->rhd/dot_general | solution.py:103
  43.9 1.7 %copy.33 = bf16[128,512]{1,0:T(8,128)(2,1)} copy(bf16[128,512]{0,1:T(8,128)(2,1)} %bitcast.58) | data formatting | bytes 262144
  45.6 7.3 %all_gather.15 = bf16[512,512]{1,0:T(8,128)(2,1)S(1)} all-gather(bf16[128,512]{1,0:T(8,128)(2,1)S(1)} %copy-done.7), channel_id=1, replica_groups=mesh['grp'=8,'blk'=4] {'blk'}, dimensions={0}, use_global_device_ids=true | all-gather | bytes 655360 | tf_op jit(solution)/shard_map/all_gather | solution.py:112
  52.8 1.0 copy.31
  53.8 9.5 %all_gather.14 = bf16[512,512]{1,0:T(8,128)(2,1)S(1)} all-gather(bf16[128,512]{1,0:T(8,128)(2,1)S(1)} %get-tuple-element.92), channel_id=1, replica_groups=mesh['grp'=8,'blk'=4] {'blk'}, dimensions={0}, use_global_device_ids=true | all-gather | bytes 655360 | tf_op jit(solution)/shard_map/all_gather | solution.py:113
  63.3 1.0 copy.29
  64.3 0.1 fusion.22
  64.5 0.0 copy-start.11
  64.5 1.6 %fusion.34 = f32[8,512,128]{2,1,0:T(8,128)S(1)} fusion(bf16[512,8,64]{0,2,1:T(8,128)(2,1)} %bitcast.48, bf16[128,8,64]{0,2,1:T(8,128)(2,1)S(1)} %bitcast.55), kind=kOutput, calls=%fused_computation.58 | convolution fusion | flops 67108864 | bytes 2752512 | tf_op jit(solution)/shard_map/while/body/eval_jaxpr/nhd,rhd->hnr/dot_general | solution.py:123
  66.2 2.6 %fusion.4 = bf16[8,128,64]{1,2,0:T(8,128)(2,1)S(1)} fusion(bf16[512,8,64]{0,2,1:T(8,128)(2,1)} %bitcast.49, f32[8,512,128]{2,1,0:T(8,128)S(1)} %fusion.34, bf16[512,8,64]{0,2,1:T(8,128)(2,1)} %bitcast.53, bf16[128,8,64]{0,2,1:T(8,128)(2,1)} %bitcast.57, f32[512,128]{1,0:T(8,128)S(1)} %fusion.22), kind=kOutput, calls=%fused_computation.11 | convolution fusion | flops 140115968 | bytes 3670016 | tf_op jit(solution)/shard_map/while/body/eval_jaxpr/hnr,nhd->rhd/dot_general | solution.py:135
  68.8 0.8 copy.34
  69.5 3.2 %reduce-scatter.2.cloned.1.call-done = f32[512,256]{1,0:T(8,128)} async-done(((f32[512,1024]{1,0:T(8,128)}), f32[512,256]{1,0:T(8,128)}) %reduce-scatter.2.cloned.1.call-update) | async-done | bytes 524304 | tf_op jit(solution)/shard_map/reduce_scatter | solution.py:146
  72.7 0.0 all-reduce.2.cloned.1.call-update
  72.7 2.0 %convolution_convert_fusion.1 = bf16[8,64,128]{2,1,0:T(8,128)(2,1)S(1)} fusion(bf16[512,8,64]{0,2,1:T(8,128)(2,1)} %bitcast.54, f32[8,512,128]{2,1,0:T(8,128)S(1)} %fusion.34, f32[512,128]{1,0:T(8,128)} %copy-done.11), kind=kOutput, calls=%fused_computation.13 | convolution fusion | flops 70844416 | bytes 3014656 | tf_op jit(solution)/shard_map/while/body/eval_jaxpr/hnr,nhd->rhd/dot_general | solution.py:138
  74.7 0.8 copy.35
  75.5 1.0 convolution_convert_fusion
  76.5 73.1 %all-reduce.2.cloned.1.call-done = f32[512,256]{1,0:T(8,128)} async-done(((f32[512,256]{1,0:T(8,128)}), f32[512,256]{1,0:T(8,128)}) %all-reduce.2.cloned.1.call-update) | async-done | bytes 524304 | tf_op jit(solution)/shard_map/psum | solution.py:147
  149.6 1.9 %copy.38 = f32[512,256]{1,0:T(8,128)} copy(f32[512,256]{1,0:T(8,128)} %all-reduce.2.cloned.1.call-done) | data formatting | bytes 1048576
  (24 shorter events, 0.1 us)
Async XLA Ops:
  7.2 25.8 %copy-start = (bf16[512,1024]{1,0:T(8,128)(2,1)S(1)}, bf16[512,1024]{1,0:T(8,128)(2,1)}, u32[]{:S(2)}) copy-start(bf16[512,1024]{1,0:T(8,128)(2,1)} %param.15) | copy-start | bytes 3145732
  7.2 65.5 %reduce-scatter.2.cloned.1.call-start = ((), (), s32[]{:S(2)}) async-start(), calls=%async_computation.1 | async-start | bytes 2621440 | tf_op jit(solution)/shard_map/reduce_scatter | solution.py:146
  27.4 3.7 %copy-start.13 = (pred[512]{0:T(512)(128)(4,1)}, pred[512]{0:T(512)(128)(4,1)S(1)}, u32[]{:S(2)}) copy-start(pred[512]{0:T(512)(128)(4,1)S(1)} %iota_compare_fusion.2) | copy-start | bytes 1540
  29.1 2.1 %copy-start.10 = (f32[128,512]{1,0:T(8,128)}, f32[128,512]{1,0:T(8,128)S(1)}, u32[]{:S(2)}) copy-start(f32[128,512]{1,0:T(8,128)S(1)} %fusion.19) | copy-start | bytes 786436
  29.1 3.9 %copy-start.9 = (bf16[128,512]{1,0:T(8,128)(2,1)S(1)}, bf16[128,512]{1,0:T(8,128)(2,1)}, u32[]{:S(2)}) copy-start(bf16[128,512]{1,0:T(8,128)(2,1)} %param.11) | copy-start | bytes 393220
  29.1 3.9 %copy-start.12 = (f32[512]{0:T(512)S(1)}, f32[512]{0:T(512)}, u32[]{:S(2)}) copy-start(f32[512]{0:T(512)} %param.14) | copy-start | bytes 6148
  31.2 0.7 copy-start.4
  33.0 4.0 %copy-start.3 = (bf16[128,1024]{1,0:T(8,128)(2,1)S(1)}, bf16[128,1024]{1,0:T(8,128)(2,1)}, u32[]{:S(2)}) copy-start(bf16[128,1024]{1,0:T(8,128)(2,1)} %param.12) | copy-start | bytes 786436
  36.4 0.6 copy-start.1
  37.0 1.9 %copy-start.5 = (bf16[128,512]{1,0:T(8,128)(2,1)S(1)}, bf16[128,512]{1,0:T(8,128)(2,1)}, u32[]{:S(2)}) copy-start(bf16[128,512]{1,0:T(8,128)(2,1)} %param.9) | copy-start | bytes 393220
  37.0 2.7 %copy-start.6 = (bf16[128,512]{1,0:T(8,128)(2,1)S(1)}, bf16[128,512]{1,0:T(8,128)(2,1)}, u32[]{:S(2)}) copy-start(bf16[128,512]{1,0:T(8,128)(2,1)} %param.10) | copy-start | bytes 393220
  38.9 110.8 %all-reduce.2.cloned.1.call-start = ((), (), s32[]{:S(2)}) async-start(), calls=%async_computation.2 | async-start | bytes 1048576 | tf_op jit(solution)/shard_map/psum | solution.py:147
  40.6 5.0 %copy-start.7 = (bf16[128,512]{1,0:T(8,128)(2,1)S(1)}, bf16[128,512]{1,0:T(8,128)(2,1)}, u32[]{:S(2)}) copy-start(bf16[128,512]{1,0:T(8,128)(2,1)} %param.8) | copy-start | bytes 393220
  43.9 20.5 %copy-start.14 = (pred[512]{0:T(512)(128)(4,1)S(1)}, pred[512]{0:T(512)(128)(4,1)}, u32[]{:S(2)}) copy-start(pred[512]{0:T(512)(128)(4,1)} %copy-done.13) | copy-start | bytes 1540
  43.9 20.6 %copy-start.8 = (bf16[128,512]{0,1:T(8,128)(2,1)S(1)}, bf16[128,512]{0,1:T(8,128)(2,1)}, u32[]{:S(2)}) copy-start(bf16[128,512]{0,1:T(8,128)(2,1)} %copy.32) | copy-start | bytes 393220
  64.5 4.3 %copy-start.11 = (f32[512,128]{1,0:T(8,128)}, f32[512,128]{1,0:T(8,128)S(1)}, u32[]{:S(2)}) copy-start(f32[512,128]{1,0:T(8,128)S(1)} %fusion.22) | copy-start | bytes 786436
  72.7 2.8 %copy-start.2 = (bf16[128,512]{1,0:T(8,128)(2,1)S(1)}, bf16[128,512]{1,0:T(8,128)(2,1)}, u32[]{:S(2)}) copy-start(bf16[128,512]{1,0:T(8,128)(2,1)} %copy-done.1) | copy-start | bytes 393220
Sparse Core Ops, SparseCore 0:
  39.0 33.6 reduce-scatter.1
  76.1 73.4 all-reduce.1
where the time goes:
time: 159 us; the launch traced here: 158 us
  waiting for transfers between devices  76.3 us (48%)
  blocking collectives  33.2 us (21%)
  matrix products  17.5 us (11%)
  between operations  14.9 us (9%)
  local copies, waits for them, and re-layouts  13.7 us (9%)
  other arithmetic  2.64 us (2%)
    psum x1, waiting for transfers between devices, shards(): grad_weight = lax.psum(column_part, 'grp')  73.1 us
    all_gather x1, blocking collectives, shards(): grad_piece = lax.all_gather(attended_grad, 'blk', axis=0, tiled=True)  9.49 us
    all_gather x1, blocking collectives, shards(): lax.all_gather(value, 'blk', axis=0, tiled=True)  8.99 us
    unnamed x37, local copies, waits for them, and re-layouts  8.42 us
    all_gather x1, blocking collectives, shards(): lax.all_gather(key, 'blk', axis=0, tiled=True)  7.49 us
    all_gather x1, blocking collectives, shards(): query_piece = lax.all_gather(query, 'blk', axis=0, tiled=True)  7.27 us
    dot_general x1, matrix products, query_step(): jnp.einsum('hrn,nhd->rhd', score_grad, key_block, preferred_element_type=...  3.29 us
  transfers between devices with their start and end apart: 2, of which 2 were waited for; matrix products, arithmetic and copies ran while one was open for 11% of the time, Pallas kernels for 0%

commit v1 on v0

--- a/solution.py
+++ b/solution.py
@@ -144,7 +144,8 @@
     grad_key = (key_acc * scale).reshape(rows, HEADS * HEAD).astype(jnp.bfloat16)
     grad_value = value_acc.reshape(rows, HEADS * HEAD).astype(jnp.bfloat16)
     column_part = lax.psum_scatter(weight_term, "blk", scatter_dimension=1, tiled=True)
-    grad_weight = lax.psum(column_part, "grp")
+    runs_search = lambda content, group_axis: jnp.sum(lax.all_gather(content, group_axis), axis=0)
+    grad_weight = runs_search(column_part, group_axis="grp")
     return (layer_out, grad_query, grad_key, grad_value, grad_gate, grad_weight)
 
 

time: 159 us -> 149 us (0.937)
  local copies, waits for them, and re-layouts: 13.7 us -> 6.69 us
  matrix products: 17.5 us -> 12.8 us
  blocking collectives: 33.2 us -> 30.2 us
  waiting for transfers between devices: 76.3 us -> 79.2 us
  other arithmetic: 2.64 us -> 4.52 us
    psum x1 -> x0, waiting for transfers between devices: 73.1 us -> none  [shards(): grad_weight = lax.psum(column_part, 'grp')]
    all_gather x0 -> x1, waiting for transfers between devices: none -> 47 us  [shards(): lax.all_gather(content, group_axis)]
    reduce_scatter x1, waiting for transfers between devices: 3.17 us -> 32.1 us  [shards(): lax.psum_scatter(weight_term, 'blk', scatter_dimension=1, tiled=True)]
    unnamed x37 -> x28, local copies, waits for them, and re-layouts: 8.42 us -> 3.99 us
    reduce_sum x0 -> x1, other arithmetic: none -> 3.31 us  [shards(): jnp.sum(lax.all_gather(content, group_axis), axis=0)]
    all_gather x1, blocking collectives: 9.49 us -> 7.27 us  [shards(): grad_piece = lax.all_gather(attended_grad, 'blk', axis=0, tiled=True)]
  transfers between devices with their start and end apart: 2 -> 2, of which waited for: 2 -> 2; matrix products, arithmetic and copies ran while one was open for 11% -> 9% of each run, Pallas kernels for 0% -> 0%
where the time goes in v1:
time: 149 us
  waiting for transfers between devices  79.2 us (53%)
  blocking collectives  30.2 us (20%)
  between operations  15 us (10%)
  matrix products  12.8 us (9%)
  local copies, waits for them, and re-layouts  6.69 us (4%)
  other arithmetic  4.52 us (3%)
    all_gather x1, waiting for transfers between devices, shards(): lax.all_gather(content, group_axis)  47 us
    reduce_scatter x1, waiting for transfers between devices, shards(): lax.psum_scatter(weight_term, 'blk', scatter_dimension=1, tiled=True)  32.1 us
    all_gather x1, blocking collectives, shards(): lax.all_gather(key, 'blk', axis=0, tiled=True)  8.86 us
    all_gather x1, blocking collectives, shards(): lax.all_gather(value, 'blk', axis=0, tiled=True)  7.49 us
    all_gather x1, blocking collectives, shards(): grad_piece = lax.all_gather(attended_grad, 'blk', axis=0, tiled=True)  7.27 us
    all_gather x1, blocking collectives, shards(): query_piece = lax.all_gather(query, 'blk', axis=0, tiled=True)  6.61 us
    unnamed x28, local copies, waits for them, and re-layouts  3.99 us
    reduce_sum x1, other arithmetic, shards(): jnp.sum(lax.all_gather(content, group_axis), axis=0)  3.31 us
  transfers between devices with their start and end apart: 2, of which 2 were waited for; matrix products, arithmetic and copies ran while one was open for 9% of the time, Pallas kernels for 0%

profile of v1, /device:TPU:0, one launch (start us, length us, event | category | flops | bytes accessed | tf_op | source)
XLA Modules:
  0.0 148.5 jit_solution(10595568718587752208)
XLA Ops:
  7.2 0.0 copy-start
  7.2 0.0 reduce-scatter.2.cloned.1.call-start
  8.0 1.0 copy.24
  9.0 8.9 %all_gather.18 = bf16[512,512]{1,0:T(8,128)(2,1)S(1)} all-gather(bf16[128,512]{1,0:T(8,128)(2,1)} %param.9), channel_id=1, replica_groups=mesh['grp'=8,'blk'=4] {'blk'}, dimensions={0}, use_global_device_ids=true | all-gather | bytes 655360 | tf_op jit(solution)/shard_map/all_gather | solution.py:43
  17.9 0.2 copy.25
  18.1 7.5 %all_gather.19 = bf16[512,512]{1,0:T(8,128)(2,1)S(1)} all-gather(bf16[128,512]{1,0:T(8,128)(2,1)} %param.10), channel_id=1, replica_groups=mesh['grp'=8,'blk'=4] {'blk'}, dimensions={0}, use_global_device_ids=true | all-gather | bytes 655360 | tf_op jit(solution)/shard_map/all_gather | solution.py:44
  25.6 0.2 copy.26
  25.8 0.5 fusion.33
  26.3 0.0 copy-start.1
  26.3 0.1 fusion.19
  26.4 0.0 copy-start.8
  26.4 0.0 copy-start.2
  26.5 0.0 copy-start.7
  26.5 0.0 copy-start.10
  26.5 0.8 fusion.32
  27.3 0.3 copy-done.1
  27.6 0.1 copy-done.8
  27.7 0.1 fusion.16
  27.8 0.1 copy.27
  27.9 0.0 copy-done
  27.9 0.0 copy-done.2
  28.0 0.6 fusion.23
  28.6 0.8 multiply_convert_fusion.6
  29.4 1.8 %fusion.35 = f32[512,1024]{1,0:T(8,128)} fusion(bf16[128,512]{1,0:T(8,128)(2,1)S(1)} %get-tuple-element.93, bf16[128,1024]{1,0:T(8,128)(2,1)S(1)} %copy-done.2), kind=kOutput, calls=%fused_computation.59 | convolution fusion | flops 134217728 | bytes 2490368 | tf_op jit(solution)/shard_map/dot_general | solution.py:82
  31.2 0.0 reduce-scatter.2.cloned.1.call-update
  31.2 0.0 all-gather.3.cloned.1.call-start
  31.3 32.1 %reduce-scatter.2.cloned.1.call-done = f32[512,256]{1,0:T(8,128)} async-done(((f32[512,1024]{1,0:T(8,128)}), f32[512,256]{1,0:T(8,128)}) %reduce-scatter.2.cloned.1.call-update) | async-done | bytes 524304 | tf_op jit(solution)/shard_map/reduce_scatter | solution.py:146
  63.4 0.0 all-gather.3.cloned.1.call-update
  63.4 0.1 copy.32
  63.5 0.0 copy-done.4
  63.5 0.1 copy.30
  63.7 6.6 %all_gather.21 = bf16[512,512]{1,0:T(8,128)(2,1)S(1)} all-gather(bf16[128,512]{1,0:T(8,128)(2,1)S(1)} %copy-done.5), channel_id=1, replica_groups=mesh['grp'=8,'blk'=4] {'blk'}, dimensions={0}, use_global_device_ids=true | all-gather | bytes 655360 | tf_op jit(solution)/shard_map/all_gather | solution.py:112
  70.3 1.0 copy.31
  71.3 0.1 copy.28
  71.4 3.0 %fusion.5 = bf16[8,128,64]{1,2,0:T(8,128)(2,1)S(1)} fusion(bf16[512,8,64]{0,2,1:T(8,128)(2,1)S(1)} %bitcast.49, f32[8,128,512]{2,1,0:T(8,128)} %copy-done.1, bf16[128,8,64]{0,2,1:T(8,128)(2,1)S(1)} %bitcast.62, bf16[512,8,64]{0,2,1:T(8,128)(2,1)S(1)} %bitcast.54, f32[128,512]{1,0:T(8,128)} %copy-done.8), kind=kOutput, calls=%fused_computation.12 | convolution fusion | flops 140115968 | bytes 3670016 | tf_op jit(solution)/shard_map/while/body/eval_jaxpr/hrn,nhd->rhd/dot_general | solution.py:103
  74.4 0.8 copy.33
  75.2 7.3 %all_gather.20 = bf16[512,512]{1,0:T(8,128)(2,1)S(1)} all-gather(bf16[128,512]{1,0:T(8,128)(2,1)S(1)} %get-tuple-element.92), channel_id=1, replica_groups=mesh['grp'=8,'blk'=4] {'blk'}, dimensions={0}, use_global_device_ids=true | all-gather | bytes 655360 | tf_op jit(solution)/shard_map/all_gather | solution.py:113
  82.5 1.0 copy.29
  83.5 0.1 fusion.22
  83.6 0.0 copy-start.9
  83.6 1.7 %fusion.34 = f32[8,512,128]{2,1,0:T(8,128)S(1)} fusion(bf16[512,8,64]{0,2,1:T(8,128)(2,1)} %bitcast.50, bf16[128,8,64]{0,2,1:T(8,128)(2,1)S(1)} %bitcast.57), kind=kOutput, calls=%fused_computation.58 | convolution fusion | flops 67108864 | bytes 2752512 | tf_op jit(solution)/shard_map/while/body/eval_jaxpr/nhd,rhd->hnr/dot_general | solution.py:123
  85.3 0.8 convolution_convert_fusion.1
  86.2 0.8 copy.35
  86.9 2.6 %fusion.4 = bf16[8,128,64]{1,2,0:T(8,128)(2,1)S(1)} fusion(bf16[512,8,64]{0,2,1:T(8,128)(2,1)} %bitcast.51, f32[8,512,128]{2,1,0:T(8,128)S(1)} %fusion.34, bf16[512,8,64]{0,2,1:T(8,128)(2,1)} %bitcast.55, bf16[128,8,64]{0,2,1:T(8,128)(2,1)S(1)} %bitcast.59, f32[512,128]{1,0:T(8,128)} %copy-done.9), kind=kOutput, calls=%fused_computation.11 | convolution fusion | flops 140115968 | bytes 3670016 | tf_op jit(solution)/shard_map/while/body/eval_jaxpr/hnr,nhd->rhd/dot_general | solution.py:135
  89.6 0.8 copy.34
  90.3 1.0 convolution_convert_fusion
  91.3 47.0 %all-gather.3.cloned.1.call-done = f32[4096,256]{1,0:T(8,128)} async-done(((f32[512,256]{1,0:T(8,128)}), f32[4096,256]{1,0:T(8,128)}) %all-gather.3.cloned.1.call-update) | async-done | bytes 4194320 | tf_op jit(solution)/shard_map/all_gather | solution.py:147
  138.4 3.3 %reduce_sum.49 = f32[512,256]{1,0:T(8,128)} reduce(f32[8,512,256]{2,1,0:T(8,128)} %bitcast.47, f32[]{:T(128)} %constant.45.clone.1), dimensions={0}, to_apply=%region_5.6 | reduce | flops 917504 | bytes 4718596 | tf_op jit(solution)/shard_map/reduce_sum | solution.py:147
  (16 shorter events, 0.1 us)
Async XLA Ops:
  7.2 20.8 %copy-start = (bf16[512,1024]{1,0:T(8,128)(2,1)S(1)}, bf16[512,1024]{1,0:T(8,128)(2,1)}, u32[]{:S(2)}) copy-start(bf16[512,1024]{1,0:T(8,128)(2,1)} %param.15) | copy-start | bytes 3145732
  7.2 56.2 %reduce-scatter.2.cloned.1.call-start = ((), (), s32[]{:S(2)}) async-start(), calls=%async_computation.1 | async-start | bytes 2621440 | tf_op jit(solution)/shard_map/reduce_scatter | solution.py:146
  26.3 1.3 copy-start.1
  26.4 1.3 copy-start.8
  26.4 1.5 %copy-start.2 = (bf16[128,1024]{1,0:T(8,128)(2,1)S(1)}, bf16[128,1024]{1,0:T(8,128)(2,1)}, u32[]{:S(2)}) copy-start(bf16[128,1024]{1,0:T(8,128)(2,1)} %param.12) | copy-start | bytes 786436
  26.5 1.5 %copy-start.7 = (bf16[128,512]{1,0:T(8,128)(2,1)S(1)}, bf16[128,512]{1,0:T(8,128)(2,1)}, u32[]{:S(2)}) copy-start(bf16[128,512]{1,0:T(8,128)(2,1)} %param.11) | copy-start | bytes 393220
  26.5 1.5 %copy-start.10 = (f32[512]{0:T(512)S(1)}, f32[512]{0:T(512)}, u32[]{:S(2)}) copy-start(f32[512]{0:T(512)} %param.14) | copy-start | bytes 6148
  29.4 34.0 %copy-start.3 = (bf16[128,512]{1,0:T(8,128)(2,1)S(1)}, bf16[128,512]{1,0:T(8,128)(2,1)}, u32[]{:S(2)}) copy-start(bf16[128,512]{1,0:T(8,128)(2,1)} %param.9) | copy-start | bytes 393220
  29.4 34.1 %copy-start.4 = (bf16[128,512]{1,0:T(8,128)(2,1)S(1)}, bf16[128,512]{1,0:T(8,128)(2,1)}, u32[]{:S(2)}) copy-start(bf16[128,512]{1,0:T(8,128)(2,1)} %param.10) | copy-start | bytes 393220
  31.2 32.5 %copy-start.5 = (bf16[128,512]{1,0:T(8,128)(2,1)S(1)}, bf16[128,512]{1,0:T(8,128)(2,1)}, u32[]{:S(2)}) copy-start(bf16[128,512]{1,0:T(8,128)(2,1)} %param.8) | copy-start | bytes 393220
  31.2 107.1 %all-gather.3.cloned.1.call-start = ((), (), s32[]{:S(2)}) async-start(), calls=%async_computation.2 | async-start | bytes 4718592 | tf_op jit(solution)/shard_map/all_gather | solution.py:147
  83.5 1.8 %copy-start.6 = (bf16[512,512]{0,1:T(8,128)(2,1)S(1)}, bf16[512,512]{0,1:T(8,128)(2,1)}, u32[]{:S(2)}) copy-start(bf16[512,512]{0,1:T(8,128)(2,1)} %copy.29) | copy-start | bytes 1572868
  83.6 2.5 %copy-start.9 = (f32[512,128]{1,0:T(8,128)}, f32[512,128]{1,0:T(8,128)S(1)}, u32[]{:S(2)}) copy-start(f32[512,128]{1,0:T(8,128)S(1)} %fusion.22) | copy-start | bytes 786436
Sparse Core Ops, SparseCore 0:
  31.3 31.9 reduce-scatter.1
  65.5 72.8 all-gather.2
